TPU v7x, 32 devices: a whole 2x2x4 slice. The times are simulated.
32 devices in a mesh: band: 8 (over y, x, core), grid: 4 (over z).
Axes of the slice: x: 2, y: 2, z: 4, core: 2. Of those that a mesh axis runs over, the one named last changes fastest.
Arguments:
- wave: bfloat16 [4096, 10240], P('band', 'grid'), may hold values from -6 to 6
- ritz: bfloat16 [4096, 4096], P('band', 'grid'), may hold values from -0.125 to 0.125
- occupation: float32 [4096], P('band'), may hold values from 0 to 2
Outputs:
- rotated: bfloat16 [4096, 10240], P('band', 'grid')
- density: float32 [10240], P('grid')
All inputs are finite; a program needn't handle non-finite values.
Results may differ from a plain program's by a relative error of at most 0.0017.
Values may be sent and summed in bfloat16 or wider, within the bound.
A program may use at most 128 MiB of HBM per device.

v0:
```python
import jax
import jax.numpy as jnp
from jax import lax
from jax.sharding import PartitionSpec as P

NB = 4096


def per_device(wave, ritz, occupation):
    ritz_rows = lax.all_gather(ritz, "grid", axis=1, tiled=True)
    ritz_cols = lax.all_to_all(ritz_rows, "band", split_axis=1, concat_axis=0, tiled=True)
    summed = lax.dot_general(
        ritz_cols,
        lax.all_gather(wave, "band", axis=0, tiled=True),
        (((0,), (0,)), ((), ())),
        preferred_element_type=jnp.float32,
    )
    rotated = summed.astype(jnp.bfloat16)
    values = rotated.astype(jnp.float32)
    partial_terms = jnp.sum(occupation[:, None] * values * values, axis=0)
    density = lax.psum(partial_terms, "band") / NB
    return (rotated, density)


def solution(mesh):
    return jax.shard_map(
        per_device,
        mesh=mesh,
        in_specs=(P("band", "grid"), P("band", "grid"), P("band")),
        out_specs=(P("band", "grid"), P("grid")),
        check_vma=False,
    )
```

profile of v0, /device:TPU:0, one launch (start us, length us, event | category | flops | bytes accessed | tf_op | source)
XLA Modules:
  0.0 287.0 jit_solution(8882897534836297578)
XLA Ops:
  7.2 0.0 all-gather.3.cloned.1.call-start
  7.2 2.3 copy.5
  9.5 0.0 all-gather.3.cloned.1.call-update
  9.5 0.0 all-gather.5.cloned.1.call-start
  9.6 0.7 all-gather.5.cloned.1.call-update
  10.3 83.3 %all-gather.3.cloned.1.call-done = bf16[512,4096]{0,1:T(8,128)(2,1)} async-done(((bf16[512,1024]{0,1:T(8,128)(2,1)}), bf16[512,4096]{0,1:T(8,128)(2,1)}) %all-gather.3.cloned.1.call-update) | async-done | bytes 4194320 | tf_op jit(solution)/shard_map/all_gather | solution.py:10
  93.6 81.7 %all_to_all.19 = bf16[512,8,512]{0,2,1:T(8,128)(2,1)} all-to-all(bf16[512,8,512]{0,2,1:T(8,128)(2,1)} %bitcast.6), channel_id=1, replica_groups=mesh['band'=8,'grid'=4] {'band'}, dimensions={1} | all-to-all | bytes 8388608 | tf_op jit(solution)/shard_map/all_to_all | solution.py:11
  175.3 0.0 copy-start
  175.3 6.8 %copy.6 = bf16[8,512,512]{2,1,0:T(8,128)(2,1)} copy(bf16[8,512,512]{1,2,0:T(8,128)(2,1)} %bitcast.5) | data formatting | bytes 8388608 | tf_op jit(solution)/shard_map/all_to_all | solution.py:11
  182.1 56.3 %all-gather.5.cloned.1.call-done = bf16[4096,2560]{1,0:T(8,128)(2,1)} async-done(((bf16[512,2560]{1,0:T(8,128)(2,1)}), bf16[4096,2560]{1,0:T(8,128)(2,1)}) %all-gather.5.cloned.1.call-update) | async-done | bytes 20971536 | tf_op jit(solution)/shard_map/all_gather | solution.py:14
  238.4 0.0 copy-done
  238.4 17.7 %fusion = (f32[2560]{0:T(1024)S(1)}, bf16[512,2560]{1,0:T(8,128)(2,1)}) fusion(f32[512]{0:T(512)S(1)} %copy-done, bf16[4096,512]{1,0:T(8,128)(2,1)} %bitcast.7, bf16[4096,2560]{1,0:T(8,128)(2,1)} %all-gather.5.cloned.1.call-done), kind=kOutput, calls=%fused_computation.1 | convolution fusion | flops 10743969792 | bytes 27799552 | tf_op jit(solution)/shard_map/dot_general | solution.py:12
  256.1 23.5 %psum.7 = f32[2560]{0:T(1024)S(1)} all-reduce(f32[2560]{0:T(1024)S(1)} %get-tuple-element.2), channel_id=1, replica_groups=mesh['band'=8,'grid'=4] {'band'}, use_global_device_ids=true, to_apply=%region_1.0 | all-reduce | flops 2560 | bytes 20480 | tf_op jit(solution)/shard_map/psum | solution.py:21
  279.5 0.6 broadcast_multiply_fusion
Async XLA Ops:
  7.2 86.4 %all-gather.3.cloned.1.call-start = ((), (), s32[]{:S(2)}) async-start(), calls=%async_computation.1 | async-start | bytes 5242880 | tf_op jit(solution)/shard_map/all_gather | solution.py:10
  9.5 228.9 %all-gather.5.cloned.1.call-start = ((), (), s32[]{:S(2)}) async-start(), calls=%async_computation.2 | async-start | bytes 23592960 | tf_op jit(solution)/shard_map/all_gather | solution.py:14
  175.3 63.1 %copy-start = (f32[512]{0:T(512)S(1)}, f32[512]{0:T(512)}, u32[]{:S(2)}) copy-start(f32[512]{0:T(512)} %param.5) | copy-start | bytes 6148
Sparse Core Ops, SparseCore 0:
  10.1 83.4 all-gather.2
  95.5 142.8 all-gather.4
where the time goes:
time: 287 us
  waiting for transfers between devices  140 us (49%)
  blocking collectives  105 us (37%)
  matrix products  17.7 us (6%)
  between operations  14 us (5%)
  local copies, waits for them, and re-layouts  9.09 us (3%)
    all_gather x1, waiting for transfers between devices, per_device(): ritz_rows = lax.all_gather(ritz, 'grid', axis=1, tiled=True)  83.3 us
    all_to_all x1, blocking collectives, per_device(): lax.all_to_all(ritz_rows, 'band', split_axis=1, concat_axis=0, tiled=True)  81.7 us
    all_gather x1, waiting for transfers between devices, per_device(): lax.all_gather(wave, 'band', axis=0, tiled=True)  56.3 us
    psum x1, blocking collectives, per_device(): density = lax.psum(partial_terms, 'band') / NB  23.5 us
    dot_general x1, matrix products, per_device(): lax.dot_general(ritz_cols, lax.all_gather(wave, 'band', axis=0, tiled=Tru...  17.7 us
    all_to_all x1, local copies, waits for them, and re-layouts, per_device(): lax.all_to_all(ritz_rows, 'band', split_axis=1, concat_axis=0, tiled=True)  6.81 us
  transfers between devices with their start and end apart: 2, of which 2 were waited for; matrix products, arithmetic and copies ran while one was open for 2% of the time, Pallas kernels for 0%

commit v1 on v0

--- a/solution.py
+++ b/solution.py
@@ -7,7 +7,22 @@
 
 
 def per_device(wave, ritz, occupation):
-    ritz_rows = lax.all_gather(ritz, "grid", axis=1, tiled=True)
+
+    def switch_terms_on(frame_in, group_axis):
+        many = lax.axis_size(group_axis)
+        carry_in = frame_in
+        tray = [carry_in]
+        it = 0
+        taken_in = [(dev_j - 1, dev_j) for dev_j in range(1, many)] + [(many - 1, 0)]
+        while it < many - 1:
+            carry_in = lax.ppermute(carry_in, group_axis, taken_in)
+            tray += [carry_in]
+            it += 1
+        res = jnp.concatenate([*reversed(tray)], 1)
+        out_arr = jnp.roll(res, (lax.axis_index(group_axis) + 1) * carry_in.shape[1], 1)
+        return out_arr
+
+    ritz_rows = switch_terms_on(ritz, "grid")
     ritz_cols = lax.all_to_all(ritz_rows, "band", split_axis=1, concat_axis=0, tiled=True)
     summed = lax.dot_general(
         ritz_cols,

time: 287 us -> 218 us (0.76)
  waiting for transfers between devices: 140 us -> 77.4 us
  blocking collectives: 105 us -> 93 us
  starting transfers between devices: 0.08 us -> 3.15 us
    all_gather x1 -> x0, waiting for transfers between devices: 83.3 us -> none  [per_device(): ritz_rows = lax.all_gather(ritz, 'grid', axis=1, tiled=True)]
    ppermute x0 -> x3, waiting for transfers between devices: none -> 76.7 us  [switch_terms_on(): carry_in = lax.ppermute(carry_in, group_axis, taken_in)]
    all_gather x1, waiting for transfers between devices: 56.3 us -> 0.01 us  [per_device(): lax.all_gather(wave, 'band', axis=0, tiled=True)]
    all_to_all x1, blocking collectives: 81.7 us -> 70.7 us  [per_device(): lax.all_to_all(ritz_rows, 'band', split_axis=1, concat_axis=0, tiled=True)]
    ppermute x0 -> x3, starting transfers between devices: none -> 3.11 us  [switch_terms_on(): carry_in = lax.ppermute(carry_in, group_axis, taken_in)]
  transfers between devices with their start and end apart: 2 -> 4, of which waited for: 2 -> 3; matrix products, arithmetic and copies ran while one was open for 2% -> 5% of each run, Pallas kernels for 0% -> 0%
where the time goes in v1:
time: 218 us; the launch traced here: 217 us
  blocking collectives  93 us (43%)
  waiting for transfers between devices  77.4 us (36%)
  matrix products  17.7 us (8%)
  between operations  14.1 us (6%)
  local copies, waits for them, and re-layouts  11.3 us (5%)
  starting transfers between devices  3.15 us (1%)
    ppermute x3, waiting for transfers between devices, switch_terms_on(): carry_in = lax.ppermute(carry_in, group_axis, taken_in)  76.7 us
    all_to_all x1, blocking collectives, per_device(): lax.all_to_all(ritz_rows, 'band', split_axis=1, concat_axis=0, tiled=True)  70.7 us
    psum x1, blocking collectives, per_device(): density = lax.psum(partial_terms, 'band') / NB  22.3 us
    dot_general x1, matrix products, per_device(): lax.dot_general(ritz_cols, lax.all_gather(wave, 'band', axis=0, tiled=Tru...  17.7 us
    all_to_all x1, local copies, waits for them, and re-layouts, per_device(): lax.all_to_all(ritz_rows, 'band', split_axis=1, concat_axis=0, tiled=True)  6.5 us
    unnamed x10, local copies, waits for them, and re-layouts  4.44 us
  transfers between devices with their start and end apart: 4, of which 3 were waited for; matrix products, arithmetic and copies ran while one was open for 5% of the time, Pallas kernels for 0%

profile of v1, /device:TPU:0, one launch (start us, length us, event | category | flops | bytes accessed | tf_op | source)
XLA Modules:
  0.0 217.2 jit_solution(4942098505358791003)
XLA Ops:
  7.2 0.0 all-gather.2.cloned.1.call-start
  7.2 0.7 all-gather.2.cloned.1.call-update
  7.9 1.5 copy.5
  9.4 3.1 %collective-permute-start = (bf16[512,1024]{0,1:T(8,128)(2,1)S(1)}, bf16[512,1024]{0,1:T(8,128)(2,1)S(1)}, u32[]{:S(2)}, u32[]{:S(2)}) collective-permute-start(bf16[512,1024]{0,1:T(8,128)(2,1)S(1)} %copy.5), channel_id=1, source_target_pairs={{0,1},{1,2},{2,3},{3,0},{4,5},{5,6},{6,7},{7,4},{8,9},{9,10},{10,1... | collective-permute-start | bytes 3145736 | tf_op jit(solution)/shard_map/ppermute | solution.py:18
  12.5 25.2 %collective-permute-done = bf16[512,1024]{0,1:T(8,128)(2,1)S(1)} collective-permute-done((bf16[512,1024]{0,1:T(8,128)(2,1)S(1)}, bf16[512,1024]{0,1:T(8,128)(2,1)S(1)}, u32[]{:S(2)}, u32[]{:S(2)}) %collective-permute-start) | collective-permute-done | bytes 1048608 | tf_op jit(solution)/shard_map/ppermute | solution.py:18
  37.7 0.0 collective-permute-start.1
  37.7 26.1 %collective-permute-done.1 = bf16[512,1024]{0,1:T(8,128)(2,1)S(1)} collective-permute-done((bf16[512,1024]{0,1:T(8,128)(2,1)S(1)}, bf16[512,1024]{0,1:T(8,128)(2,1)S(1)}, u32[]{:S(2)}, u32[]{:S(2)}) %collective-permute-start.1) | collective-permute-done | bytes 1048608 | tf_op jit(solution)/shard_map/ppermute | solution.py:18
  63.8 0.0 collective-permute-start.2
  63.8 25.4 %collective-permute-done.2 = bf16[512,1024]{0,1:T(8,128)(2,1)} collective-permute-done((bf16[512,1024]{0,1:T(8,128)(2,1)S(1)}, bf16[512,1024]{0,1:T(8,128)(2,1)}, u32[]{:S(2)}, u32[]{:S(2)}) %collective-permute-start.2) | collective-permute-done | bytes 1048608 | tf_op jit(solution)/shard_map/ppermute | solution.py:18
  89.2 1.3 constant_dynamic-update-slice_fusion.7
  90.5 0.1 constant_dynamic-update-slice_fusion.6
  90.6 0.1 constant_dynamic-update-slice_fusion.5
  90.6 0.1 constant_dynamic-update-slice_fusion.4
  90.7 1.3 constant_dynamic-update-slice_fusion.3
  92.0 0.1 constant_dynamic-update-slice_fusion.2
  92.1 0.1 constant_dynamic-update-slice_fusion.1
  92.2 0.1 constant_dynamic-update-slice_fusion
  92.2 0.3 constant_dynamic-slice_fusion
  92.5 0.0 copy-start
  92.5 70.7 %all_to_all.19 = bf16[512,8,512]{0,2,1:T(8,128)(2,1)} all-to-all(bf16[512,8,512]{0,2,1:T(8,128)(2,1)S(1)} %bitcast.5), channel_id=1, replica_groups=mesh['band'=8,'grid'=4] {'band'}, dimensions={1} | all-to-all | bytes 8388608 | tf_op jit(solution)/shard_map/all_to_all | solution.py:26
  163.2 6.5 %copy.8 = bf16[8,512,512]{2,1,0:T(8,128)(2,1)} copy(bf16[8,512,512]{1,2,0:T(8,128)(2,1)} %bitcast.6) | data formatting | bytes 8388608 | tf_op jit(solution)/shard_map/all_to_all | solution.py:26
  169.7 0.0 all-gather.2.cloned.1.call-done
  169.7 0.0 copy-done
  169.7 17.7 %fusion = (f32[2560]{0:T(1024)S(1)}, bf16[512,2560]{1,0:T(8,128)(2,1)}) fusion(f32[512]{0:T(512)S(1)} %copy-done, bf16[4096,512]{1,0:T(8,128)(2,1)} %bitcast.7, bf16[4096,2560]{1,0:T(8,128)(2,1)} %all-gather.2.cloned.1.call-done), kind=kOutput, calls=%fused_computation.1 | convolution fusion | flops 10743969792 | bytes 27799552 | tf_op jit(solution)/shard_map/dot_general | solution.py:27
  187.4 22.3 %psum.7 = f32[2560]{0:T(1024)S(1)} all-reduce(f32[2560]{0:T(1024)S(1)} %get-tuple-element.2), channel_id=1, replica_groups=mesh['band'=8,'grid'=4] {'band'}, use_global_device_ids=true, to_apply=%region_1.2 | all-reduce | flops 2560 | bytes 20480 | tf_op jit(solution)/shard_map/psum | solution.py:36
  209.8 0.6 broadcast_multiply_fusion
Async XLA Ops:
  7.2 162.6 %all-gather.2.cloned.1.call-start = ((), (), s32[]{:S(2)}) async-start(), calls=%async_computation.1 | async-start | bytes 23592960 | tf_op jit(solution)/shard_map/all_gather | solution.py:29
  9.4 28.3 %collective-permute-start = (bf16[512,1024]{0,1:T(8,128)(2,1)S(1)}, bf16[512,1024]{0,1:T(8,128)(2,1)S(1)}, u32[]{:S(2)}, u32[]{:S(2)}) collective-permute-start(bf16[512,1024]{0,1:T(8,128)(2,1)S(1)} %copy.5), channel_id=1, source_target_pairs={{0,1},{1,2},{2,3},{3,0},{4,5},{5,6},{6,7},{7,4},{8,9},{9,10},{10,1... | collective-permute-start | bytes 3145736 | tf_op jit(solution)/shard_map/ppermute | solution.py:18
  37.7 26.1 %collective-permute-start.1 = (bf16[512,1024]{0,1:T(8,128)(2,1)S(1)}, bf16[512,1024]{0,1:T(8,128)(2,1)S(1)}, u32[]{:S(2)}, u32[]{:S(2)}) collective-permute-start(bf16[512,1024]{0,1:T(8,128)(2,1)S(1)} %collective-permute-done), channel_id=1, source_target_pairs={{0,1},{1,2},{2,3},{3,0},{4,5},{5,6},{6,7},{7,4},{8,9},{9,10},{10,1... | collective-permute-start | bytes 3145736 | tf_op jit(solution)/shard_map/ppermute | solution.py:18
  63.8 25.4 %collective-permute-start.2 = (bf16[512,1024]{0,1:T(8,128)(2,1)S(1)}, bf16[512,1024]{0,1:T(8,128)(2,1)}, u32[]{:S(2)}, u32[]{:S(2)}) collective-permute-start(bf16[512,1024]{0,1:T(8,128)(2,1)S(1)} %collective-permute-done.1), channel_id=1, source_target_pairs={{0,1},{1,2},{2,3},{3,0},{4,5},{5,6},{6,7},{7,4},{8,9},{9,10},{10,1... | collective-permute-start | bytes 3145736 | tf_op jit(solution)/shard_map/ppermute | solution.py:18
  92.5 77.2 %copy-start = (f32[512]{0:T(512)S(1)}, f32[512]{0:T(512)}, u32[]{:S(2)}) copy-start(f32[512]{0:T(512)} %param.5) | copy-start | bytes 6148
Sparse Core Ops, SparseCore 0:
  9.9 145.3 all-gather.1

commit v2 on v0

--- a/solution.py
+++ b/solution.py
@@ -18,7 +18,7 @@
     rotated = summed.astype(jnp.bfloat16)
     values = rotated.astype(jnp.float32)
     partial_terms = jnp.sum(occupation[:, None] * values * values, axis=0)
-    density = lax.psum(partial_terms, "band") / NB
+    density = jnp.sum(lax.all_gather(partial_terms, axis_name="band"), axis=0) / NB
     return (rotated, density)
 
 

time: 287 us -> 273 us (0.951)
  blocking collectives: 105 us -> 90.9 us
    psum x1 -> x0, blocking collectives: 23.5 us -> none  [per_device(): density = lax.psum(partial_terms, 'band') / NB]
    all_gather x0 -> x1, blocking collectives: none -> 9.24 us  [per_device(): lax.all_gather(partial_terms, axis_name='band')]
where the time goes in v2:
time: 273 us
  waiting for transfers between devices  140 us (51%)
  blocking collectives  90.9 us (33%)
  matrix products  17.7 us (6%)
  between operations  14 us (5%)
  local copies, waits for them, and re-layouts  9.1 us (3%)
    all_gather x1, waiting for transfers between devices, per_device(): ritz_rows = lax.all_gather(ritz, 'grid', axis=1, tiled=True)  83.3 us
    all_to_all x1, blocking collectives, per_device(): lax.all_to_all(ritz_rows, 'band', split_axis=1, concat_axis=0, tiled=True)  81.7 us
    all_gather x1, waiting for transfers between devices, per_device(): lax.all_gather(wave, 'band', axis=0, tiled=True)  56.3 us
    dot_general x1, matrix products, per_device(): lax.dot_general(ritz_cols, lax.all_gather(wave, 'band', axis=0, tiled=Tru...  17.7 us
    all_gather x1, blocking collectives, per_device(): lax.all_gather(partial_terms, axis_name='band')  9.24 us
    all_to_all x1, local copies, waits for them, and re-layouts, per_device(): lax.all_to_all(ritz_rows, 'band', split_axis=1, concat_axis=0, tiled=True)  6.81 us
  transfers between devices with their start and end apart: 2, of which 2 were waited for; matrix products, arithmetic and copies ran while one was open for 2% of the time, Pallas kernels for 0%

profile of v2, /device:TPU:0, one launch (start us, length us, event | category | flops | bytes accessed | tf_op | source)
XLA Modules:
  0.0 272.8 jit_solution(13163691572105657755)
XLA Ops:
  7.2 0.0 all-gather.5.cloned.1.call-start
  7.2 2.3 copy.7
  9.5 0.0 all-gather.5.cloned.1.call-update
  9.5 0.0 all-gather.7.cloned.1.call-start
  9.6 0.7 all-gather.7.cloned.1.call-update
  10.3 83.3 %all-gather.5.cloned.1.call-done = bf16[512,4096]{0,1:T(8,128)(2,1)} async-done(((bf16[512,1024]{0,1:T(8,128)(2,1)}), bf16[512,4096]{0,1:T(8,128)(2,1)}) %all-gather.5.cloned.1.call-update) | async-done | bytes 4194320 | tf_op jit(solution)/shard_map/all_gather | solution.py:10
  93.6 81.7 %all_to_all.19 = bf16[512,8,512]{0,2,1:T(8,128)(2,1)} all-to-all(bf16[512,8,512]{0,2,1:T(8,128)(2,1)} %bitcast.6), channel_id=1, replica_groups=mesh['band'=8,'grid'=4] {'band'}, dimensions={1} | all-to-all | bytes 8388608 | tf_op jit(solution)/shard_map/all_to_all | solution.py:11
  175.3 0.0 copy-start
  175.3 6.8 %copy.8 = bf16[8,512,512]{2,1,0:T(8,128)(2,1)} copy(bf16[8,512,512]{1,2,0:T(8,128)(2,1)} %bitcast.5) | data formatting | bytes 8388608 | tf_op jit(solution)/shard_map/all_to_all | solution.py:11
  182.1 56.3 %all-gather.7.cloned.1.call-done = bf16[4096,2560]{1,0:T(8,128)(2,1)} async-done(((bf16[512,2560]{1,0:T(8,128)(2,1)}), bf16[4096,2560]{1,0:T(8,128)(2,1)}) %all-gather.7.cloned.1.call-update) | async-done | bytes 20971536 | tf_op jit(solution)/shard_map/all_gather | solution.py:14
  238.4 0.0 copy-done
  238.4 17.7 %fusion = (f32[2560]{0:T(1024)S(1)}, bf16[512,2560]{1,0:T(8,128)(2,1)}) fusion(f32[512]{0:T(512)S(1)} %copy-done, bf16[4096,512]{1,0:T(8,128)(2,1)} %bitcast.7, bf16[4096,2560]{1,0:T(8,128)(2,1)} %all-gather.7.cloned.1.call-done), kind=kOutput, calls=%fused_computation.1 | convolution fusion | flops 10743969792 | bytes 27799552 | tf_op jit(solution)/shard_map/dot_general | solution.py:12
  256.1 9.2 %all-gather.1 = f32[8,1,2560]{2,1,0:T(1,128)S(1)} all-gather(f32[1,1,2560]{2,1,0:T(1,128)S(1)} %reshape.9), channel_id=2, replica_groups=mesh['band'=8,'grid'=4] {'band'}, dimensions={0}, use_global_device_ids=true | all-gather | bytes 92160 | tf_op jit(solution)/shard_map/all_gather | solution.py:21
  265.3 0.1 reduce_sum.19
  265.4 0.6 broadcast_multiply_fusion
  (1 shorter events, 0.0 us)
Async XLA Ops:
  7.2 86.4 %all-gather.5.cloned.1.call-start = ((), (), s32[]{:S(2)}) async-start(), calls=%async_computation.1 | async-start | bytes 5242880 | tf_op jit(solution)/shard_map/all_gather | solution.py:10
  9.5 228.9 %all-gather.7.cloned.1.call-start = ((), (), s32[]{:S(2)}) async-start(), calls=%async_computation.2 | async-start | bytes 23592960 | tf_op jit(solution)/shard_map/all_gather | solution.py:14
  175.3 63.1 %copy-start = (f32[512]{0:T(512)S(1)}, f32[512]{0:T(512)}, u32[]{:S(2)}) copy-start(f32[512]{0:T(512)} %param.5) | copy-start | bytes 6148
Sparse Core Ops, SparseCore 0:
  10.1 83.4 all-gather.4
  95.5 142.8 all-gather.6
